TPU v7x, 512 devices: a whole 4x8x8 slice. The times are simulated.
512 devices in a mesh: expert: 128 (over x, z, y_lo), hidden: 4 (over y_hi, core).
Axes of the slice: x: 4, y: 8 (y_hi: 2, y_lo: 4; y = y_hi * 4 + y_lo), z: 8, core: 2. Of those that a mesh axis runs over, the one named last changes fastest.
Arguments:
- tokens: bfloat16 [512, 196, 1024], P(('expert', 'hidden')), may hold values from -40 to 40
- router: bfloat16 [1024, 128], replicated, may hold values from -0.5 to 0.5
- w_in: bfloat16 [128, 1024, 3072], P('expert', None, 'hidden'), may hold values from -0.1875 to 0.1875
- b_in: float32 [128, 3072], P('expert', 'hidden'), may hold values from -6 to 6
- w_out: bfloat16 [128, 3072, 1024], P('expert', 'hidden'), may hold values from -0.109375 to 0.109375
- cotangent: bfloat16 [512, 196, 1024], P(('expert', 'hidden')), may hold values from -6 to 6
Outputs:
- mixed: bfloat16 [512, 196, 1024], P(('expert', 'hidden'))
- token_grad: bfloat16 [512, 196, 1024], P(('expert', 'hidden'))
All inputs are finite; a program needn't handle non-finite values.
Results may differ from a plain program's by a relative error of at most 0.015.
Values may be sent and summed in bfloat16 or wider, within the bound.
No kernel may reach another device: no remote copies, remote signals or barrier semaphores. Data moves between devices by JAX's collectives and lax.ppermute only.
A program may use at most 64 MiB of HBM per device.

v0:
```python
import jax
import jax.numpy as jnp
from jax import lax
from jax.sharding import PartitionSpec as P


def split_up(x, dim, devices):
    shape = x.shape
    parts = x.reshape(*shape[:dim], devices, shape[dim] // devices, *shape[dim + 1 :])
    return jnp.moveaxis(parts, dim, 0)


def sum_at_owner(x, axis, dim):
    devices = lax.axis_size(axis)
    parts = lax.all_to_all(split_up(x, dim, devices), axis, 0, 0, tiled=True)
    return jnp.sum(parts.astype(jnp.float32), axis=0)


def outbound(stacked):
    moved = lax.all_to_all(stacked, "expert", split_axis=2, concat_axis=1, tiled=True)
    return lax.all_gather(moved, "hidden", axis=1, tiled=True)


def inbound(terms):
    summed = sum_at_owner(terms.astype(jnp.bfloat16), "hidden", 1)
    return lax.all_to_all(
        summed.astype(jnp.bfloat16), "expert", split_axis=1, concat_axis=2, tiled=True
    )


def expert_forward(slots, w_in, b_in, w_out):
    pre = jnp.einsum("red,edf->ref", slots, w_in, preferred_element_type=jnp.float32) + b_in[None]
    act = jax.nn.gelu(pre).astype(jnp.bfloat16)
    return (jnp.einsum("ref,efd->red", act, w_out, preferred_element_type=jnp.float32), pre)


def expert_backward(grads, pre, w_in, w_out):
    act_grad = jnp.einsum("red,efd->ref", grads, w_out, preferred_element_type=jnp.float32)
    _, pull = jax.vjp(jax.nn.gelu, pre)
    pre_grad = pull(act_grad)[0].astype(jnp.bfloat16)
    return jnp.einsum("ref,edf->red", pre_grad, w_in, preferred_element_type=jnp.float32)


def shards(tokens, router, w_in, b_in, w_out, cotangent):
    logits = jnp.einsum("bmd,ds->bms", tokens, router, preferred_element_type=jnp.float32)
    dispatch = jax.nn.softmax(logits, axis=1)
    combine = jax.nn.softmax(logits, axis=2)
    dispatch_w = dispatch.astype(jnp.bfloat16)
    combine_w = combine.astype(jnp.bfloat16)
    slot_in = jnp.einsum(
        "bms,bmd->bsd", dispatch_w, tokens, preferred_element_type=jnp.float32
    ).astype(jnp.bfloat16)
    slot_cot = jnp.einsum(
        "bms,bmd->bsd", combine_w, cotangent, preferred_element_type=jnp.float32
    ).astype(jnp.bfloat16)
    arrived = outbound(jnp.stack([slot_in, slot_cot]))
    partial_value, pre = expert_forward(arrived[0], w_in, b_in, w_out)
    gpartial = expert_backward(arrived[1], pre, w_in, w_out)
    returned = inbound(jnp.stack([partial_value, gpartial]))
    slot_out = returned[0]
    slot_grad = returned[1]
    mixed = jnp.einsum(
        "bms,bsd->bmd", combine_w, slot_out, preferred_element_type=jnp.float32
    ).astype(jnp.bfloat16)
    combine_grad = jnp.einsum(
        "bmd,bsd->bms", cotangent, slot_out, preferred_element_type=jnp.float32
    )
    dispatch_grad = jnp.einsum(
        "bmd,bsd->bms", tokens, slot_grad, preferred_element_type=jnp.float32
    )
    logit_grad = combine * (combine_grad - jnp.sum(combine * combine_grad, axis=2, keepdims=True))
    logit_grad = logit_grad + dispatch * (
        dispatch_grad - jnp.sum(dispatch * dispatch_grad, axis=1, keepdims=True)
    )
    logit_grad = logit_grad.astype(jnp.bfloat16)
    token_grad = jnp.einsum(
        "bms,bsd->bmd", dispatch_w, slot_grad, preferred_element_type=jnp.float32
    )
    token_grad = token_grad + jnp.einsum(
        "bms,ds->bmd", logit_grad, router, preferred_element_type=jnp.float32
    )
    return (mixed, token_grad.astype(jnp.bfloat16))


def solution(mesh):
    return jax.shard_map(
        shards,
        mesh=mesh,
        in_specs=(
            P(("expert", "hidden"), None, None),
            P(),
            P("expert", None, "hidden"),
            P("expert", "hidden"),
            P("expert", "hidden", None),
            P(("expert", "hidden"), None, None),
        ),
        out_specs=(P(("expert", "hidden"), None, None), P(("expert", "hidden"), None, None)),
        check_vma=False,
    )
```

profile of v0, /device:TPU:1, one launch (start us, length us, event | category | flops | bytes accessed | tf_op | source)
XLA Modules:
  0.0 200.0 jit_solution(14822342059811094486)
XLA Ops:
  7.2 0.0 copy-start
  7.2 0.0 copy-start.3
  7.2 0.0 all-gather.3.cloned.1.call-start
  7.2 1.6 fusion.82
  8.8 0.2 fusion.59
  9.0 1.3 fusion.35
  10.3 0.0 copy-done.3
  10.3 0.4 fusion.36
  10.7 0.1 pad_maximum_fusion
  10.7 0.5 copy.17
  11.3 0.0 copy-start.4
  11.3 37.1 %all_to_all.26 = bf16[2,1,128,1024]{3,0,1,2:T(2,128)(2,1)S(1)} all-to-all(bf16[2,1,128,1024]{3,0,1,2:T(2,128)(2,1)S(1)} %copy.17), channel_id=1, replica_groups=mesh['expert'=128,'hidden'=4] {'expert'}, dimensions={2} | all-to-all | bytes 1048576 | tf_op jit(solution)/shard_map/all_to_all | solution.py:20
  48.4 0.9 copy.18
  49.3 0.0 all-gather.3.cloned.1.call-update
  49.3 0.0 copy-done.4
  49.4 39.7 %all-gather.3.cloned.1.call-done = bf16[2,1,512,1024]{3,2,1,0:T(8,128)(2,1)} async-done(((bf16[2,1,128,1024]{3,2,1,0:T(8,128)(2,1)}), bf16[2,1,512,1024]{3,2,1,0:T(8,128)(2,1)}) %all-gather.3.cloned.1.call-update) | async-done | bytes 2097168 | tf_op jit(solution)/shard_map/all_gather | solution.py:21
  89.1 2.7 %fusion.7 = f32[512,1,768]{2,0,1:T(8,128)S(1)} fusion(bf16[1,1024,768]{2,1,0:T(8,128)(2,1)} %param.8, bf16[2,1,512,1024]{3,2,1,0:T(8,128)(2,1)} %all-gather.3.cloned.1.call-done, f32[768]{0:T(1024)S(1)} %reduce.14), kind=kOutput, calls=%fused_computation.11 | convolution fusion | flops 805699584 | bytes 4197376 | tf_op jit(solution)/shard_map/red,edf->ref/dot_general | solution.py:32
  91.8 0.0 copy-start.5
  91.8 1.1 copy-done.5
  92.9 0.0 copy-done
  92.9 1.1 fusion.22
  94.1 6.1 %fusion.19 = bf16[512,1024]{1,0:T(8,128)(2,1)} fusion(bf16[1,1024,768]{2,1,0:T(8,128)(2,1)} %param.8, f32[512,1,768]{2,0,1:T(8,128)} %copy-done.5, bf16[1,768,1024]{2,1,0:T(8,128)(2,1)S(1)} %copy-done, bf16[2,1,512,1024]{3,2,1,0:T(8,128)(2,1)} %all-gather.3.cloned.1.call-done), kind=kOutput, calls=%fused_computation.26 | convolution fusion | flops 1619001344 | bytes 6815744 | tf_op jit(solution)/shard_map/ref,edf->red/dot_general | solution.py:41
  100.1 1.4 maximum_bitcast_fusion
  101.5 45.0 %all_to_all.27 = bf16[4,2,128,1,1024]{4,2,3,1,0:T(8,128)(2,1)} all-to-all(bf16[4,2,128,1,1024]{4,2,3,1,0:T(8,128)(2,1)S(1)} %maximum_bitcast_fusion), channel_id=1, replica_groups=mesh['expert'=128,'hidden'=4] {'hidden'}, dimensions={0} | all-to-all | bytes 4194304 | tf_op jit(solution)/shard_map/all_to_all | solution.py:15
  146.6 2.0 %reduce_sum.52 = bf16[2,128,1024]{2,1,0:T(8,128)(2,1)S(1)} reduce(bf16[4,2,128,1,1024]{4,2,3,1,0:T(8,128)(2,1)} %all_to_all.27, bf16[]{:T(256)} %constant.19.clone.1), dimensions={0,3}, to_apply=%region_4.0 | reduce | flops 786432 | bytes 2621442 | tf_op jit(solution)/shard_map/reduce_sum | solution.py:16
  148.6 0.5 copy.21
  149.1 0.0 copy-start.1
  149.2 40.0 %all_to_all.28 = bf16[2,128,1,1024]{3,0,2,1:T(2,128)(2,1)S(1)} all-to-all(bf16[2,128,1,1024]{3,0,2,1:T(2,128)(2,1)S(1)} %copy.21), channel_id=1, replica_groups=mesh['expert'=128,'hidden'=4] {'expert'}, dimensions={1} | all-to-all | bytes 1048576 | tf_op jit(solution)/shard_map/all_to_all | solution.py:26
  189.2 0.7 fusion.83
  189.9 0.0 copy-done.1
  189.9 0.3 convolution_bitcast_fusion
  190.2 0.0 copy-start.2
  190.2 0.3 fusion.55
  190.5 1.1 fusion.34
  191.6 0.4 multiply_reduce_fusion.1
  192.0 0.0 copy-done.2
  192.0 1.1 fusion.33
  (1 shorter events, 0.0 us)
Async XLA Ops:
  7.2 85.8 %copy-start = (bf16[1,768,1024]{2,1,0:T(8,128)(2,1)S(1)}, bf16[1,768,1024]{2,1,0:T(8,128)(2,1)}, u32[]{:S(2)}) copy-start(bf16[1,768,1024]{2,1,0:T(8,128)(2,1)} %param.10) | copy-start | bytes 4718596
  7.2 3.1 %copy-start.3 = (bf16[1,196,1024]{2,1,0:T(8,128)(2,1)S(1)}, bf16[1,196,1024]{2,1,0:T(8,128)(2,1)}, u32[]{:S(2)}) copy-start(bf16[1,196,1024]{2,1,0:T(8,128)(2,1)} %param.11) | copy-start | bytes 1204228
  7.2 81.9 %all-gather.3.cloned.1.call-start = ((), (), s32[]{:S(2)}) async-start(), calls=%async_computation.3 | async-start | bytes 2621440 | tf_op jit(solution)/shard_map/all_gather | solution.py:21
  11.3 38.1 %copy-start.4 = (f32[1,768]{1,0:T(1,128)S(1)}, f32[1,768]{1,0:T(1,128)}, u32[]{:S(2)}) copy-start(f32[1,768]{1,0:T(1,128)} %param.9) | copy-start | bytes 9220
  91.8 1.2 copy-start.5
  149.1 40.8 %copy-start.1 = (bf16[1,196,1024]{2,1,0:T(8,128)(2,1)S(1)}, bf16[1,196,1024]{2,1,0:T(8,128)(2,1)}, u32[]{:S(2)}) copy-start(bf16[1,196,1024]{2,1,0:T(8,128)(2,1)} %param.6) | copy-start | bytes 1204228
  190.2 1.8 copy-start.2
Sparse Core Ops, SparseCore 0:
  49.5 39.5 all-gather.2
where the time goes:
time: 200 us
  blocking collectives  122 us (61%)
  waiting for transfers between devices  39.7 us (20%)
  matrix products  16.2 us (8%)
  between operations  14.2 us (7%)
  local copies, waits for them, and re-layouts  3.9 us (2%)
  other arithmetic  3.7 us (2%)
    all_to_all x1, blocking collectives, sum_at_owner(): parts = lax.all_to_all(split_up(x, dim, devices), axis, 0, 0, tiled=True)  45 us
    all_to_all x1, blocking collectives, inbound(): lax.all_to_all(summed.astype(jnp.bfloat16), 'expert', split_axis=1, conca...  40 us
    all_gather x1, waiting for transfers between devices, outbound(): return lax.all_gather(moved, 'hidden', axis=1, tiled=True)  39.7 us
    all_to_all x1, blocking collectives, outbound(): lax.all_to_all(stacked, 'expert', split_axis=2, concat_axis=1, tiled=True)  37.1 us
    dot_general x1, matrix products, expert_backward(): jnp.einsum('ref,edf->red', pre_grad, w_in, preferred_element_type=jnp.flo...  6.06 us
  transfers between devices with their start and end apart: 1, of which 1 were waited for; matrix products, arithmetic and copies ran while one was open for 0% of the time, Pallas kernels for 0%

commit v1 on v0

--- a/solution.py
+++ b/solution.py
@@ -18,7 +18,7 @@
 
 def outbound(stacked):
     moved = lax.all_to_all(stacked, "expert", split_axis=2, concat_axis=1, tiled=True)
-    return lax.all_gather(moved, "hidden", axis=1, tiled=True)
+    return jnp.concatenate(lax.all_gather(moved, "hidden"), axis=1)
 
 
 def inbound(terms):

time: 200 us -> 201 us (level)
  no operation moved by 1% of the time
where the time goes in v1:
time: 201 us; the launch traced here: 200 us
  blocking collectives  122 us (61%)
  waiting for transfers between devices  39.7 us (20%)
  matrix products  15.2 us (8%)
  between operations  14.2 us (7%)
  local copies, waits for them, and re-layouts  4.8 us (2%)
  other arithmetic  4.02 us (2%)
    all_to_all x1, blocking collectives, sum_at_owner(): parts = lax.all_to_all(split_up(x, dim, devices), axis, 0, 0, tiled=True)  45 us
    all_to_all x1, blocking collectives, inbound(): lax.all_to_all(summed.astype(jnp.bfloat16), 'expert', split_axis=1, conca...  40 us
    all_gather x1, waiting for transfers between devices, outbound(): return jnp.concatenate(lax.all_gather(moved, 'hidden'), axis=1)  39.7 us
    all_to_all x1, blocking collectives, outbound(): lax.all_to_all(stacked, 'expert', split_axis=2, concat_axis=1, tiled=True)  37.1 us
    dot_general x1, matrix products, expert_backward(): jnp.einsum('ref,edf->red', pre_grad, w_in, preferred_element_type=jnp.flo...  5.78 us
  transfers between devices with their start and end apart: 1, of which 1 were waited for; matrix products, arithmetic and copies ran while one was open for 0% of the time, Pallas kernels for 0%

profile of v1, /device:TPU:1, one launch (start us, length us, event | category | flops | bytes accessed | tf_op | source)
XLA Modules:
  0.0 200.2 jit_solution(16117053878484089036)
XLA Ops:
  7.2 0.0 copy-start
  7.2 0.0 copy-start.3
  7.2 0.0 all-gather.3.cloned.1.call-start
  7.2 1.6 fusion.82
  8.8 0.2 fusion.59
  9.0 1.3 fusion.35
  10.3 0.0 copy-done.3
  10.3 0.4 fusion.36
  10.7 0.1 pad_maximum_fusion
  10.7 0.5 copy.18
  11.3 0.0 copy-start.4
  11.3 37.1 %all_to_all.23 = bf16[2,1,128,1024]{3,0,1,2:T(2,128)(2,1)S(1)} all-to-all(bf16[2,1,128,1024]{3,0,1,2:T(2,128)(2,1)S(1)} %copy.18), channel_id=1, replica_groups=mesh['expert'=128,'hidden'=4] {'expert'}, dimensions={2} | all-to-all | bytes 1048576 | tf_op jit(solution)/shard_map/all_to_all | solution.py:20
  48.4 0.9 copy.19
  49.3 0.0 all-gather.3.cloned.1.call-update
  49.3 0.0 copy-done.4
  49.4 39.7 %all-gather.3.cloned.1.call-done = bf16[8,1,128,1024]{3,2,1,0:T(8,128)(2,1)} async-done(((bf16[2,1,128,1024]{3,2,1,0:T(8,128)(2,1)}), bf16[8,1,128,1024]{3,2,1,0:T(8,128)(2,1)}) %all-gather.3.cloned.1.call-update) | async-done | bytes 2097168 | tf_op jit(solution)/shard_map/all_gather | solution.py:21
  89.1 0.0 copy-start.5
  89.1 1.8 fusion.83
  90.9 0.2 copy-done.5
  91.1 1.0 fusion.7
  92.1 0.0 copy-done
  92.1 0.0 copy-start.6
  92.1 2.1 %fusion.22 = bf16[512,1024]{1,0:T(8,128)(2,1)} fusion(bf16[1,768,1024]{2,1,0:T(8,128)(2,1)S(1)} %copy-done, f32[512,1,768]{2,0,1:T(8,128)S(1)} %fusion.7), kind=kOutput, calls=%fused_computation.27 | convolution fusion | flops 809369600 | bytes 4194304 | tf_op jit(solution)/shard_map/ref,efd->red/dot_general | solution.py:34
  94.2 0.0 copy-done.6
  94.2 5.8 %fusion.19 = bf16[512,1024]{1,0:T(8,128)(2,1)} fusion(bf16[1,1024,768]{2,1,0:T(8,128)(2,1)} %param.8, f32[512,1,768]{2,0,1:T(8,128)} %copy-done.6, bf16[512,1024]{1,0:T(8,128)(2,1)S(1)} %bitcast.128, bf16[1,768,1024]{2,1,0:T(8,128)(2,1)S(1)} %copy-done), kind=kOutput, calls=%fused_computation.26 | convolution fusion | flops 1619001344 | bytes 6815744 | tf_op jit(solution)/shard_map/ref,edf->red/dot_general | solution.py:41
  100.0 1.7 maximum_bitcast_fusion
  101.8 45.0 %all_to_all.24 = bf16[4,2,128,1,1024]{4,2,3,1,0:T(8,128)(2,1)} all-to-all(bf16[4,2,128,1,1024]{4,2,3,1,0:T(8,128)(2,1)S(1)} %maximum_bitcast_fusion), channel_id=1, replica_groups=mesh['expert'=128,'hidden'=4] {'hidden'}, dimensions={0} | all-to-all | bytes 4194304 | tf_op jit(solution)/shard_map/all_to_all | solution.py:15
  146.8 2.0 %reduce_sum.52 = bf16[2,128,1024]{2,1,0:T(8,128)(2,1)S(1)} reduce(bf16[4,2,128,1,1024]{4,2,3,1,0:T(8,128)(2,1)} %all_to_all.24, bf16[]{:T(256)} %constant.19.clone.1), dimensions={0,3}, to_apply=%region_4.0 | reduce | flops 786432 | bytes 2621442 | tf_op jit(solution)/shard_map/reduce_sum | solution.py:16
  148.8 0.5 copy.22
  149.4 0.0 copy-start.1
  149.4 40.0 %all_to_all.25 = bf16[2,128,1,1024]{3,0,2,1:T(2,128)(2,1)S(1)} all-to-all(bf16[2,128,1,1024]{3,0,2,1:T(2,128)(2,1)S(1)} %copy.22), channel_id=1, replica_groups=mesh['expert'=128,'hidden'=4] {'expert'}, dimensions={1} | all-to-all | bytes 1048576 | tf_op jit(solution)/shard_map/all_to_all | solution.py:26
  189.4 0.7 fusion.84
  190.1 0.0 copy-done.1
  190.2 0.3 convolution_bitcast_fusion
  190.4 0.0 copy-start.2
  190.5 0.3 fusion.55
  190.7 1.1 fusion.34
  191.8 0.4 multiply_reduce_fusion.1
  192.2 0.0 copy-done.2
  192.2 1.1 fusion.33
  (1 shorter events, 0.0 us)
Async XLA Ops:
  7.2 84.9 %copy-start = (bf16[1,768,1024]{2,1,0:T(8,128)(2,1)S(1)}, bf16[1,768,1024]{2,1,0:T(8,128)(2,1)}, u32[]{:S(2)}) copy-start(bf16[1,768,1024]{2,1,0:T(8,128)(2,1)} %param.10) | copy-start | bytes 4718596
  7.2 3.1 %copy-start.3 = (bf16[1,196,1024]{2,1,0:T(8,128)(2,1)S(1)}, bf16[1,196,1024]{2,1,0:T(8,128)(2,1)}, u32[]{:S(2)}) copy-start(bf16[1,196,1024]{2,1,0:T(8,128)(2,1)} %param.11) | copy-start | bytes 1204228
  7.2 81.9 %all-gather.3.cloned.1.call-start = ((), (), s32[]{:S(2)}) async-start(), calls=%async_computation.3 | async-start | bytes 2621440 | tf_op jit(solution)/shard_map/all_gather | solution.py:21
  11.3 38.1 %copy-start.4 = (f32[1,768]{1,0:T(1,128)S(1)}, f32[1,768]{1,0:T(1,128)}, u32[]{:S(2)}) copy-start(f32[1,768]{1,0:T(1,128)} %param.9) | copy-start | bytes 9220
  89.1 2.0 %copy-start.5 = (bf16[1,1024,768]{2,1,0:T(8,128)(2,1)S(1)}, bf16[1,1024,768]{2,1,0:T(8,128)(2,1)}, u32[]{:S(2)}) copy-start(bf16[1,1024,768]{2,1,0:T(8,128)(2,1)} %param.8) | copy-start | bytes 4718596
  92.1 2.1 %copy-start.6 = (f32[512,1,768]{2,0,1:T(8,128)}, f32[512,1,768]{2,0,1:T(8,128)S(1)}, u32[]{:S(2)}) copy-start(f32[512,1,768]{2,0,1:T(8,128)S(1)} %fusion.7) | copy-start | bytes 4718596
  149.4 40.8 %copy-start.1 = (bf16[1,196,1024]{2,1,0:T(8,128)(2,1)S(1)}, bf16[1,196,1024]{2,1,0:T(8,128)(2,1)}, u32[]{:S(2)}) copy-start(bf16[1,196,1024]{2,1,0:T(8,128)(2,1)} %param.6) | copy-start | bytes 1204228
  190.4 1.8 copy-start.2
Sparse Core Ops, SparseCore 0:
  49.5 39.5 all-gather.2
